TPU v7x, 32 devices: a whole 2x2x4 slice. The times are simulated.
32 devices in a mesh: role: 2 (over core), rep: 4 (over z), tp: 4 (over y, x).
Axes of the slice: x: 2, y: 2, z: 4, core: 2. Of those that a mesh axis runs over, the one named last changes fastest.
Arguments:
- pre_act: bfloat16 [2, 2, 64, 14784], P('role', None, 'rep', 'tp'), may hold values from -6 to 6
- next_pre: bfloat16 [2, 2, 64, 14784], P('role', None, 'rep', 'tp'), may hold values from -6 to 6
- stream: bfloat16 [2, 2, 64, 8192], P('role', None, 'tp', 'rep'), may hold values from -6 to 6
- cotangent: bfloat16 [64, 8192], P('tp', 'rep'), may hold values from -6 to 6
- weights: float32 [2, 14784, 8192], P('role', 'tp', 'rep'), may hold values from -6 to 6
- first_moment: float32 [14784, 8192], P('tp', 'rep'), may hold values from -0.18 to 0.18
- second_moment: float32 [14784, 8192], P('tp', 'rep'), may hold values from 0.0001 to 0.001
- tree_parent: int32 [2, 64], P('role', 'tp'), may hold values from 0 to 63, as said below
- tree_depth: int32 [2, 64], P('role', 'tp'), may hold values from 1 to 16, as said below
Outputs:
- first_out: bfloat16 [2, 64, 8192], P('role', 'tp', 'rep')
- next_out: bfloat16 [2, 64, 8192], P('role', 'tp', 'rep')
- new_weights: float32 [2, 14784, 8192], P('role', 'tp', 'rep')
Inputs may be any that keep to these rules, and one draw needn't show every extreme that they name: `tree_parent`: each entry names a first-pass row of the same group that lies in the same aligned block of 16 rows as the entry's own row. `tree_depth`: one more than the depth of the named parent in its block's first-pass tree; in that tree every row but the block's first names an earlier row of the block as parent, and the first row has depth 0.
All inputs are finite; a program needn't handle non-finite values.
Results may differ from a plain program's by a relative error of at most 0.0041.
Values may be sent and summed in bfloat16 or wider, within the bound.
No kernel may reach another device: no remote copies, remote signals or barrier semaphores. Data moves between devices by JAX's collectives and lax.ppermute only.
A program may use at most 256 MiB of HBM per device.

v0:
```python
import jax
import jax.numpy as jnp
from jax import lax
from jax.sharding import PartitionSpec as P

FF = 14784
beta_one = 0.9
beta_two = 0.95
epsilon = 1e-08
learn_rate = 0.08
decay_rate = 0.1
correct_one = 1.0 - 0.9**60
correct_two = 1.0 - 0.95**60


def shifted(value, axis, by):
    size = lax.axis_size(axis)
    pairs = [(i, i + by) for i in range(size) if 0 <= i + by < size]
    return lax.ppermute(value, axis, pairs)


def activate(both_halves):
    return (
        jax.nn.silu(both_halves[0].astype(jnp.float32)) * both_halves[1].astype(jnp.float32)
    ).astype(jnp.bfloat16)


def adam_step(master, moment_one, moment_two, gradient):
    moment_one = beta_one * moment_one + (1.0 - beta_one) * gradient
    moment_two = beta_two * moment_two + (1.0 - beta_two) * gradient * gradient
    direction = moment_one / correct_one / (jnp.sqrt(moment_two / correct_two) + epsilon)
    return master - learn_rate * (direction + decay_rate * master)


def local(
    pre_act,
    next_pre,
    stream,
    cotangent,
    weights,
    first_moment,
    second_moment,
    tree_parent,
    tree_depth,
):
    learner = lax.axis_index("role") == 0
    factor = FF ** (-0.5)
    hidden = activate(pre_act[0])
    upcoming = activate(next_pre[0])
    older = weights[0].astype(jnp.bfloat16)
    cot_rows = lax.all_gather(cotangent, "tp", axis=0, tiled=True)
    width_ff, width_d = older.shape
    empty_grad = jnp.zeros((width_ff, width_d), jnp.float32)
    gradient = empty_grad
    segment = lax.all_gather(hidden, "rep", axis=0, tiled=True)
    piece = segment
    contribute_partial_value = piece

    def accumulate(held_sum):
        return lax.dot_general(
            segment, cot_rows, (((0,), (0,)), ((), ())), preferred_element_type=jnp.float32
        )

    gradient = lax.cond(learner, accumulate, lambda held_sum: held_sum, gradient)
    partial_value, gradient = (contribute_partial_value, gradient)
    summed = lax.psum_scatter(
        jnp.dot(partial_value, older, preferred_element_type=jnp.float32),
        "tp",
        scatter_dimension=0,
        tiled=True,
    )
    first_out = (stream[0, 0].astype(jnp.float32) + factor * summed).astype(jnp.bfloat16)
    updated = adam_step(weights[0], first_moment, second_moment, factor * gradient)
    fresh = updated.astype(jnp.bfloat16)
    pushed = shifted(fresh, "role", 1)
    current = jnp.where(learner, fresh, pushed)
    new_weights = jnp.where(learner, updated, pushed.astype(jnp.float32))
    piece = lax.all_gather(upcoming, "rep", axis=0, tiled=True)
    next_summed = lax.psum_scatter(
        jnp.dot(piece, current, preferred_element_type=jnp.float32),
        "tp",
        scatter_dimension=0,
        tiled=True,
    )
    block_rows = first_out.shape[0]
    local_parent = tree_parent[0] - lax.axis_index("tp") * block_rows
    onehot = (local_parent[:, None] == jnp.arange(block_rows, dtype=jnp.int32)[None, :]).astype(
        jnp.bfloat16
    )
    picked = jnp.dot(onehot, first_out, preferred_element_type=jnp.float32)
    portion = 1.0 / (1.0 + tree_depth[0].astype(jnp.float32))
    total = stream[0, 1].astype(jnp.float32) + factor * next_summed + picked * portion[:, None]
    next_out = total.astype(jnp.bfloat16)
    return (first_out[None], next_out[None], new_weights[None])


def solution(mesh):
    placed = (
        P("role", None, "rep", "tp"),
        P("role", None, "rep", "tp"),
        P("role", None, "tp", "rep"),
        P("tp", "rep"),
        P("role", "tp", "rep"),
        P("tp", "rep"),
        P("tp", "rep"),
        P("role", "tp"),
        P("role", "tp"),
    )
    return jax.shard_map(
        local,
        mesh=mesh,
        in_specs=placed,
        out_specs=(P("role", "tp", "rep"), P("role", "tp", "rep"), P("role", "tp", "rep")),
        check_vma=False,
    )
```

profile of v0, /device:TPU:0, one launch (start us, length us, event | category | flops | bytes accessed | tf_op | source)
XLA Modules:
  0.0 193.4 jit_solution(9640457482474888950)
XLA Ops:
  7.2 0.0 reduce-scatter.3.cloned.1.call-start
  7.2 1.0 fusion.15
  8.3 16.9 %all_gather.9 = bf16[64,3696]{1,0:T(8,128)(2,1)S(1)} all-gather(bf16[16,3696]{1,0:T(8,128)(2,1)S(1)} %fusion.15), channel_id=1, replica_groups=mesh['role'=2,'rep'=4,'tp'=4] {'rep'}, dimensions={0}, use_global_device_ids=true | all-gather | bytes 591360 | tf_op jit(solution)/shard_map/all_gather | solution.py:55
  25.2 9.3 %all_gather.11 = bf16[64,2048]{1,0:T(8,128)(2,1)S(1)} all-gather(bf16[16,2048]{1,0:T(8,128)(2,1)} %param.14), channel_id=1, replica_groups=mesh['role'=2,'rep'=4,'tp'=4] {'tp'}, dimensions={0}, use_global_device_ids=true | all-gather | bytes 327680 | tf_op jit(solution)/shard_map/all_gather | solution.py:51
  34.5 12.8 %conditional.1 = (f32[3696,2048]{1,0:T(8,128)}) conditional(s32[]{:T(128)} %convert_element_type.85, () %tuple.14, (bf16[64,3696]{1,0:T(8,128)(2,1)S(1)}, bf16[64,2048]{1,0:T(8,128)(2,1)S(1)}) %tuple.15), branch_computations={%region_1.2_spmd, %region_2.3_spmd} | conditional | flops 968884224 | bytes 31012872 | solution.py:64
  34.5 12.8 %fusion.28 = f32[3696,2048]{1,0:T(8,128)} fusion(bf16[64,3696]{1,0:T(8,128)(2,1)S(1)} %get-tuple-element.4, bf16[64,2048]{1,0:T(8,128)(2,1)S(1)} %get-tuple-element.8), kind=kOutput, calls=%fused_computation.39 | convolution fusion | flops 968884224 | bytes 31012864 | tf_op jit(solution)/shard_map/cond/branch_1_fun/dot_general | solution.py:60
  47.3 54.7 %fusion.24 = (bf16[3696,2048]{1,0:T(8,128)(2,1)}, f32[3696,2048]{1,0:T(8,128)}) fusion(f32[3696,2048]{1,0:T(8,128)} %get-tuple-element.16, f32[3696,2048]{1,0:T(8,128)} %param.17, f32[3696,2048]{1,0:T(8,128)} %param.16, f32[1,3696,2048]{2,1,0:T(8,128)} %param.15), kind=kLoop, calls=%fused_computation.36 | loop fusion | flops 128679936 | bytes 166526976 | tf_op jit(solution)/shard_map/convert_element_type | solution.py:74
  101.9 0.0 copy-start.4
  101.9 0.0 copy-start.1
  101.9 6.8 %collective-permute-start = (bf16[3696,2048]{1,0:T(8,128)(2,1)}, bf16[3696,2048]{1,0:T(8,128)(2,1)}, u32[]{:S(2)}, u32[]{:S(2)}) collective-permute-start(bf16[3696,2048]{1,0:T(8,128)(2,1)} %get-tuple-element.12), channel_id=1, source_target_pairs={{0,16},{1,17},{2,18},{3,19},{4,20},{5,21},{6,22},{7,23},{8,24},{9,... | collective-permute-start | bytes 45416456 | tf_op jit(solution)/shard_map/ppermute | solution.py:19
  108.7 13.1 %fusion.25 = f32[64,2048]{1,0:T(8,128)} fusion(bf16[64,3696]{1,0:T(8,128)(2,1)S(1)} %all_gather.9, f32[1,3696,2048]{2,1,0:T(8,128)} %param.15), kind=kOutput, calls=%fused_computation.37 | convolution fusion | flops 968884224 | bytes 31275008 | tf_op jit(solution)/shard_map/dot_general | solution.py:67
  121.9 0.0 reduce-scatter.3.cloned.1.call-update
  121.9 0.0 reduce-scatter.5.cloned.1.call-start
  121.9 0.0 copy-done.2
  121.9 0.1 fusion.14
  122.0 15.1 %all_gather.10 = bf16[64,3696]{1,0:T(8,128)(2,1)S(1)} all-gather(bf16[16,3696]{1,0:T(8,128)(2,1)S(1)} %fusion.14), channel_id=1, replica_groups=mesh['role'=2,'rep'=4,'tp'=4] {'rep'}, dimensions={0}, use_global_device_ids=true | all-gather | bytes 591360 | tf_op jit(solution)/shard_map/all_gather | solution.py:78
  137.1 0.0 copy-done.3
  137.1 10.8 %reduce-scatter.3.cloned.1.call-done = f32[16,2048]{1,0:T(8,128)} async-done(((f32[64,2048]{1,0:T(8,128)}), f32[16,2048]{1,0:T(8,128)}) %reduce-scatter.3.cloned.1.call-update) | async-done | bytes 131088 | tf_op jit(solution)/shard_map/reduce_scatter | solution.py:66
  147.9 1.1 convolution_multiply_fusion
  149.0 0.0 collective-permute-done
  149.0 8.9 %fusion.3 = f32[64,2048]{1,0:T(8,128)} fusion(bf16[64,3696]{1,0:T(8,128)(2,1)S(1)} %all_gather.10, bf16[3696,2048]{1,0:T(8,128)(2,1)} %get-tuple-element.12, bf16[3696,2048]{1,0:T(8,128)(2,1)} %collective-permute-done, pred[]{:T(512)S(6)} %eq.16), kind=kOutput, calls=%fused_computation.7 | convolution fusion | flops 976453632 | bytes 31275008 | tf_op jit(solution)/shard_map/dot_general | solution.py:80
  157.9 0.0 reduce-scatter.5.cloned.1.call-update
  158.0 27.0 %select_bitcast_fusion = f32[1,3696,2048]{2,1,0:T(8,128)} fusion(f32[3696,2048]{1,0:T(8,128)} %get-tuple-element.13, bf16[3696,2048]{1,0:T(8,128)(2,1)} %collective-permute-done, pred[]{:T(512)S(6)} %eq.16), kind=kLoop, calls=%fused_computation.5 | loop fusion | flops 15138816 | bytes 75694080 | tf_op jit(solution)/shard_map/broadcast_in_dim | solution.py:94
  184.9 1.6 fusion.19
  (9 shorter events, 0.0 us)
Async XLA Ops:
  7.2 140.7 %reduce-scatter.3.cloned.1.call-start = ((), (), s32[]{:S(2)}) async-start(), calls=%async_computation.2 | async-start | bytes 655360 | tf_op jit(solution)/shard_map/reduce_scatter | solution.py:66
  101.9 20.0 %copy-start.2 = (bf16[1,2,16,3696]{3,2,1,0:T(8,128)(2,1)S(1)}, bf16[1,2,16,3696]{3,2,1,0:T(8,128)(2,1)}, u32[]{:S(2)}) copy-start(bf16[1,2,16,3696]{3,2,1,0:T(8,128)(2,1)} %param.12) | copy-start | bytes 709636
  101.9 35.2 %copy-start.3 = (s32[1,16]{1,0:T(1,128)S(1)}, s32[1,16]{1,0:T(1,128)}, u32[]{:S(2)}) copy-start(s32[1,16]{1,0:T(1,128)} %param.19) | copy-start | bytes 196
  101.9 35.2 %copy-start.4 = (s32[1,16]{1,0:T(1,128)S(1)}, s32[1,16]{1,0:T(1,128)}, u32[]{:S(2)}) copy-start(s32[1,16]{1,0:T(1,128)} %param.18) | copy-start | bytes 196
  101.9 46.0 %copy-start.1 = (bf16[1,2,16,2048]{3,2,1,0:T(8,128)(2,1)S(1)}, bf16[1,2,16,2048]{3,2,1,0:T(8,128)(2,1)}, u32[]{:S(2)}) copy-start(bf16[1,2,16,2048]{3,2,1,0:T(8,128)(2,1)} %param.13) | copy-start | bytes 393220
  101.9 47.1 %collective-permute-start = (bf16[3696,2048]{1,0:T(8,128)(2,1)}, bf16[3696,2048]{1,0:T(8,128)(2,1)}, u32[]{:S(2)}, u32[]{:S(2)}) collective-permute-start(bf16[3696,2048]{1,0:T(8,128)(2,1)} %get-tuple-element.12), channel_id=1, source_target_pairs={{0,16},{1,17},{2,18},{3,19},{4,20},{5,21},{6,22},{7,23},{8,24},{9,... | collective-permute-start | bytes 45416456 | tf_op jit(solution)/shard_map/ppermute | solution.py:19
  121.9 63.1 %reduce-scatter.5.cloned.1.call-start = ((), (), s32[]{:S(2)}) async-start(), calls=%async_computation.3 | async-start | bytes 655360 | tf_op jit(solution)/shard_map/reduce_scatter | solution.py:79
  157.9 27.0 %copy-start = (f32[16,2048]{1,0:T(8,128)S(1)}, f32[16,2048]{1,0:T(8,128)}, u32[]{:S(2)}) copy-start(f32[16,2048]{1,0:T(8,128)} %reduce-scatter.3.cloned.1.call-done) | copy-start | bytes 393220
Sparse Core Ops, SparseCore 0:
  122.0 25.8 reduce-scatter.2
  158.1 25.0 reduce-scatter.4
where the time goes:
time: 194 us; the launch traced here: 193 us
  other arithmetic  84.4 us (44%)
  blocking collectives  41.3 us (21%)
  matrix products  35.9 us (19%)
  between operations  14.1 us (7%)
  waiting for transfers between devices  10.8 us (6%)
  starting transfers between devices  6.85 us (4%)
    convert_element_type x1, other arithmetic, local(): fresh = updated.astype(jnp.bfloat16)  54.7 us
    broadcast_in_dim x2, other arithmetic, local(): return (first_out[None], next_out[None], new_weights[None])  28.6 us
    all_gather x1, blocking collectives, local(): segment = lax.all_gather(hidden, 'rep', axis=0, tiled=True)  16.9 us
    all_gather x1, blocking collectives, local(): piece = lax.all_gather(upcoming, 'rep', axis=0, tiled=True)  15.1 us
    dot_general x1, matrix products, local(): jnp.dot(partial_value, older, preferred_element_type=jnp.float32)  13.1 us
    dot_general x1, matrix products, accumulate(): lax.dot_general(segment, cot_rows, (((0,), (0,)), ((), ())), preferred_el...  12.8 us
    reduce_scatter x1, waiting for transfers between devices, local(): lax.psum_scatter(jnp.dot(partial_value, older, preferred_element_type=jnp...  10.8 us
    all_gather x1, blocking collectives, local(): cot_rows = lax.all_gather(cotangent, 'tp', axis=0, tiled=True)  9.28 us
  transfers between devices with their start and end apart: 3, of which 1 were waited for; matrix products, arithmetic and copies ran while one was open for 21% of the time, Pallas kernels for 0%

commit v1 on v0

--- a/solution.py
+++ b/solution.py
@@ -75,7 +75,12 @@
     pushed = shifted(fresh, "role", 1)
     current = jnp.where(learner, fresh, pushed)
     new_weights = jnp.where(learner, updated, pushed.astype(jnp.float32))
-    piece = lax.all_gather(upcoming, "rep", axis=0, tiled=True)
+    ring = [upcoming]
+    for hop in range(3):
+        ring.append(lax.ppermute(ring[-1], "rep", [(dev, (dev + 1) % 4) for dev in range(4)]))
+    piece = jnp.roll(
+        jnp.concatenate(ring[::-1], axis=0), (lax.axis_index("rep") + 1) * ring[0].shape[0], axis=0
+    )
     next_summed = lax.psum_scatter(
         jnp.dot(piece, current, preferred_element_type=jnp.float32),
         "tp",

time: 194 us -> 195 us (level)
  blocking collectives: 41.3 us -> 26.2 us
  waiting for transfers between devices: 10.8 us -> 24 us
  starting transfers between devices: 6.85 us -> 9.11 us
    all_gather x1 -> x0, blocking collectives: 15.1 us -> none  [local(): piece = lax.all_gather(upcoming, 'rep', axis=0, tiled=True)]
    ppermute x0 -> x3, waiting for transfers between devices: none -> 13.2 us  [local(): lax.ppermute(ring[-1], 'rep', [(dev, (dev + 1) % 4) for dev in range(4)])]
    ppermute x0 -> x3, starting transfers between devices: none -> 2.26 us  [local(): lax.ppermute(ring[-1], 'rep', [(dev, (dev + 1) % 4) for dev in range(4)])]
  transfers between devices with their start and end apart: 3 -> 6, of which waited for: 1 -> 3; matrix products, arithmetic and copies ran while one was open for 21% -> 21% of each run, Pallas kernels for 0% -> 0%
where the time goes in v1:
time: 195 us; the launch traced here: 194 us
  other arithmetic  84.6 us (43%)
  matrix products  36 us (18%)
  blocking collectives  26.2 us (13%)
  waiting for transfers between devices  24 us (12%)
  between operations  14.1 us (7%)
  starting transfers between devices  9.11 us (5%)
    convert_element_type x1, other arithmetic, local(): fresh = updated.astype(jnp.bfloat16)  54.7 us
    broadcast_in_dim x2, other arithmetic, local(): return (first_out[None], next_out[None], new_weights[None])  28.6 us
    all_gather x1, blocking collectives, local(): segment = lax.all_gather(hidden, 'rep', axis=0, tiled=True)  16.9 us
    ppermute x3, waiting for transfers between devices, local(): lax.ppermute(ring[-1], 'rep', [(dev, (dev + 1) % 4) for dev in range(4)])  13.2 us
    dot_general x1, matrix products, local(): jnp.dot(partial_value, older, preferred_element_type=jnp.float32)  13.1 us
    dot_general x1, matrix products, accumulate(): lax.dot_general(segment, cot_rows, (((0,), (0,)), ((), ())), preferred_el...  12.8 us
    reduce_scatter x1, waiting for transfers between devices, local(): lax.psum_scatter(jnp.dot(partial_value, older, preferred_element_type=jnp...  10.7 us
    all_gather x1, blocking collectives, local(): cot_rows = lax.all_gather(cotangent, 'tp', axis=0, tiled=True)  9.28 us
  transfers between devices with their start and end apart: 6, of which 3 were waited for; matrix products, arithmetic and copies ran while one was open for 21% of the time, Pallas kernels for 0%

profile of v1, /device:TPU:0, one launch (start us, length us, event | category | flops | bytes accessed | tf_op | source)
XLA Modules:
  0.0 194.2 jit_solution(6375727286473032811)
XLA Ops:
  7.2 0.0 reduce-scatter.3.cloned.1.call-start
  7.2 1.0 fusion.16
  8.3 16.9 %all_gather.6 = bf16[64,3696]{1,0:T(8,128)(2,1)S(1)} all-gather(bf16[16,3696]{1,0:T(8,128)(2,1)S(1)} %fusion.16), channel_id=1, replica_groups=mesh['role'=2,'rep'=4,'tp'=4] {'rep'}, dimensions={0}, use_global_device_ids=true | all-gather | bytes 591360 | tf_op jit(solution)/shard_map/all_gather | solution.py:55
  25.2 9.3 %all_gather.7 = bf16[64,2048]{1,0:T(8,128)(2,1)S(1)} all-gather(bf16[16,2048]{1,0:T(8,128)(2,1)} %param.14), channel_id=1, replica_groups=mesh['role'=2,'rep'=4,'tp'=4] {'tp'}, dimensions={0}, use_global_device_ids=true | all-gather | bytes 327680 | tf_op jit(solution)/shard_map/all_gather | solution.py:51
  34.5 12.8 %conditional.1 = (f32[3696,2048]{1,0:T(8,128)}) conditional(s32[]{:T(128)} %convert_element_type.85, () %tuple.14, (bf16[64,3696]{1,0:T(8,128)(2,1)S(1)}, bf16[64,2048]{1,0:T(8,128)(2,1)S(1)}) %tuple.15), branch_computations={%region_1.2_spmd, %region_2.3_spmd} | conditional | flops 968884224 | bytes 31012872 | solution.py:64
  34.5 12.8 %fusion.30 = f32[3696,2048]{1,0:T(8,128)} fusion(bf16[64,3696]{1,0:T(8,128)(2,1)S(1)} %get-tuple-element.4, bf16[64,2048]{1,0:T(8,128)(2,1)S(1)} %get-tuple-element.8), kind=kOutput, calls=%fused_computation.49 | convolution fusion | flops 968884224 | bytes 31012864 | tf_op jit(solution)/shard_map/cond/branch_1_fun/dot_general | solution.py:60
  47.3 54.7 %fusion.26 = (bf16[3696,2048]{1,0:T(8,128)(2,1)}, f32[3696,2048]{1,0:T(8,128)}) fusion(f32[3696,2048]{1,0:T(8,128)} %get-tuple-element.16, f32[3696,2048]{1,0:T(8,128)} %param.17, f32[3696,2048]{1,0:T(8,128)} %param.16, f32[1,3696,2048]{2,1,0:T(8,128)} %param.15), kind=kLoop, calls=%fused_computation.46 | loop fusion | flops 128679936 | bytes 166526976 | tf_op jit(solution)/shard_map/convert_element_type | solution.py:74
  102.0 6.8 %collective-permute-start.3 = (bf16[3696,2048]{1,0:T(8,128)(2,1)}, bf16[3696,2048]{1,0:T(8,128)(2,1)}, u32[]{:S(2)}, u32[]{:S(2)}) collective-permute-start(bf16[3696,2048]{1,0:T(8,128)(2,1)} %get-tuple-element.12), channel_id=1, source_target_pairs={{0,16},{1,17},{2,18},{3,19},{4,20},{5,21},{6,22},{7,23},{8,24},{9,... | collective-permute-start | bytes 45416456 | tf_op jit(solution)/shard_map/ppermute | solution.py:19
  108.8 0.1 fusion.15
  108.9 2.2 %collective-permute-start = (bf16[16,3696]{1,0:T(8,128)(2,1)S(1)}, bf16[16,3696]{1,0:T(8,128)(2,1)S(1)}, u32[]{:S(2)}, u32[]{:S(2)}) collective-permute-start(bf16[16,3696]{1,0:T(8,128)(2,1)S(1)} %fusion.15), channel_id=1, source_target_pairs={{0,4},{4,8},{8,12},{12,0},{1,5},{5,9},{9,13},{13,1},{2,6},{6,10},{... | collective-permute-start | bytes 354824 | tf_op jit(solution)/shard_map/ppermute | solution.py:80
  111.0 13.1 %fusion.27 = f32[64,2048]{1,0:T(8,128)} fusion(bf16[64,3696]{1,0:T(8,128)(2,1)S(1)} %all_gather.6, f32[1,3696,2048]{2,1,0:T(8,128)} %param.15), kind=kOutput, calls=%fused_computation.47 | convolution fusion | flops 968884224 | bytes 31275008 | tf_op jit(solution)/shard_map/dot_general | solution.py:67
  124.2 0.0 reduce-scatter.3.cloned.1.call-update
  124.2 0.0 reduce-scatter.5.cloned.1.call-start
  124.3 0.1 collective-permute-start.1
  124.4 6.6 %collective-permute-done.1 = bf16[16,3696]{1,0:T(8,128)(2,1)S(1)} collective-permute-done((bf16[16,3696]{1,0:T(8,128)(2,1)S(1)}, bf16[16,3696]{1,0:T(8,128)(2,1)S(1)}, u32[]{:S(2)}, u32[]{:S(2)}) %collective-permute-start.1) | collective-permute-done | bytes 118304 | tf_op jit(solution)/shard_map/ppermute | solution.py:80
  131.0 6.6 %collective-permute-done.2 = bf16[16,3696]{1,0:T(8,128)(2,1)S(1)} collective-permute-done((bf16[16,3696]{1,0:T(8,128)(2,1)S(1)}, bf16[16,3696]{1,0:T(8,128)(2,1)S(1)}, u32[]{:S(2)}, u32[]{:S(2)}) %collective-permute-start.2) | collective-permute-done | bytes 118304 | tf_op jit(solution)/shard_map/ppermute | solution.py:80
  137.7 0.1 constant_dynamic-update-slice_fusion.4
  137.8 0.1 constant_dynamic-update-slice_fusion
  137.9 10.7 %reduce-scatter.3.cloned.1.call-done = f32[16,2048]{1,0:T(8,128)} async-done(((f32[64,2048]{1,0:T(8,128)}), f32[16,2048]{1,0:T(8,128)}) %reduce-scatter.3.cloned.1.call-update) | async-done | bytes 131088 | tf_op jit(solution)/shard_map/reduce_scatter | solution.py:66
  148.6 1.1 convolution_multiply_fusion
  149.7 9.0 %fusion.3 = f32[64,2048]{1,0:T(8,128)} fusion(bf16[3696,2048]{1,0:T(8,128)(2,1)} %get-tuple-element.12, bf16[3696,2048]{1,0:T(8,128)(2,1)} %collective-permute-done.3, pred[]{:T(512)S(6)} %eq.19, bf16[128,3696]{1,0:T(8,128)(2,1)S(1)} %constant_dynamic-update-slice_fusion, s32[]{:T(128)S(6)} %select_n.28), kind=kOutput, calls=%fused_computation.7 | convolution fusion | flops 976453632 | bytes 31277060 | tf_op jit(solution)/shard_map/dot_general | solution.py:85
  158.7 0.0 reduce-scatter.5.cloned.1.call-update
  158.8 27.0 %select_bitcast_fusion = f32[1,3696,2048]{2,1,0:T(8,128)} fusion(f32[3696,2048]{1,0:T(8,128)} %get-tuple-element.13, bf16[3696,2048]{1,0:T(8,128)(2,1)} %collective-permute-done.3, pred[]{:T(512)S(6)} %eq.19), kind=kLoop, calls=%fused_computation.5 | loop fusion | flops 15138816 | bytes 75694080 | tf_op jit(solution)/shard_map/broadcast_in_dim | solution.py:99
  185.7 1.6 fusion.20
  (22 shorter events, 0.1 us)
Async XLA Ops:
  7.2 141.5 %reduce-scatter.3.cloned.1.call-start = ((), (), s32[]{:S(2)}) async-start(), calls=%async_computation.2 | async-start | bytes 655360 | tf_op jit(solution)/shard_map/reduce_scatter | solution.py:66
  47.2 61.5 %copy-start = (bf16[1,2,16,3696]{3,2,1,0:T(8,128)(2,1)S(1)}, bf16[1,2,16,3696]{3,2,1,0:T(8,128)(2,1)}, u32[]{:S(2)}) copy-start(bf16[1,2,16,3696]{3,2,1,0:T(8,128)(2,1)} %param.12) | copy-start | bytes 709636
  102.0 22.4 %copy-start.3 = (s32[1,16]{1,0:T(1,128)S(1)}, s32[1,16]{1,0:T(1,128)}, u32[]{:S(2)}) copy-start(s32[1,16]{1,0:T(1,128)} %param.19) | copy-start | bytes 196
  102.0 29.0 %copy-start.4 = (s32[1,16]{1,0:T(1,128)S(1)}, s32[1,16]{1,0:T(1,128)}, u32[]{:S(2)}) copy-start(s32[1,16]{1,0:T(1,128)} %param.18) | copy-start | bytes 196
  102.0 46.6 %copy-start.2 = (bf16[1,2,16,2048]{3,2,1,0:T(8,128)(2,1)S(1)}, bf16[1,2,16,2048]{3,2,1,0:T(8,128)(2,1)}, u32[]{:S(2)}) copy-start(bf16[1,2,16,2048]{3,2,1,0:T(8,128)(2,1)} %param.13) | copy-start | bytes 393220
  102.0 47.7 %collective-permute-start.3 = (bf16[3696,2048]{1,0:T(8,128)(2,1)}, bf16[3696,2048]{1,0:T(8,128)(2,1)}, u32[]{:S(2)}, u32[]{:S(2)}) collective-permute-start(bf16[3696,2048]{1,0:T(8,128)(2,1)} %get-tuple-element.12), channel_id=1, source_target_pairs={{0,16},{1,17},{2,18},{3,19},{4,20},{5,21},{6,22},{7,23},{8,24},{9,... | collective-permute-start | bytes 45416456 | tf_op jit(solution)/shard_map/ppermute | solution.py:19
  108.9 15.4 %collective-permute-start = (bf16[16,3696]{1,0:T(8,128)(2,1)S(1)}, bf16[16,3696]{1,0:T(8,128)(2,1)S(1)}, u32[]{:S(2)}, u32[]{:S(2)}) collective-permute-start(bf16[16,3696]{1,0:T(8,128)(2,1)S(1)} %fusion.15), channel_id=1, source_target_pairs={{0,4},{4,8},{8,12},{12,0},{1,5},{5,9},{9,13},{13,1},{2,6},{6,10},{... | collective-permute-start | bytes 354824 | tf_op jit(solution)/shard_map/ppermute | solution.py:80
  124.2 61.5 %reduce-scatter.5.cloned.1.call-start = ((), (), s32[]{:S(2)}) async-start(), calls=%async_computation.3 | async-start | bytes 655360 | tf_op jit(solution)/shard_map/reduce_scatter | solution.py:84
  124.3 6.7 %collective-permute-start.1 = (bf16[16,3696]{1,0:T(8,128)(2,1)S(1)}, bf16[16,3696]{1,0:T(8,128)(2,1)S(1)}, u32[]{:S(2)}, u32[]{:S(2)}) collective-permute-start(bf16[16,3696]{1,0:T(8,128)(2,1)S(1)} %collective-permute-done), channel_id=1, source_target_pairs={{0,4},{4,8},{8,12},{12,0},{1,5},{5,9},{9,13},{13,1},{2,6},{6,10},{... | collective-permute-start | bytes 354824 | tf_op jit(solution)/shard_map/ppermute | solution.py:80
  131.0 6.6 %collective-permute-start.2 = (bf16[16,3696]{1,0:T(8,128)(2,1)S(1)}, bf16[16,3696]{1,0:T(8,128)(2,1)S(1)}, u32[]{:S(2)}, u32[]{:S(2)}) collective-permute-start(bf16[16,3696]{1,0:T(8,128)(2,1)S(1)} %collective-permute-done.1), channel_id=1, source_target_pairs={{0,4},{4,8},{8,12},{12,0},{1,5},{5,9},{9,13},{13,1},{2,6},{6,10},{... | collective-permute-start | bytes 354824 | tf_op jit(solution)/shard_map/ppermute | solution.py:80
  158.7 27.0 %copy-start.1 = (f32[16,2048]{1,0:T(8,128)S(1)}, f32[16,2048]{1,0:T(8,128)}, u32[]{:S(2)}) copy-start(f32[16,2048]{1,0:T(8,128)} %reduce-scatter.3.cloned.1.call-done) | copy-start | bytes 393220
Sparse Core Ops, SparseCore 0:
  124.3 24.2 reduce-scatter.2
  158.9 25.1 reduce-scatter.4
